TPU v7x, 32 devices: a whole 2x2x4 slice. The times are simulated.
32 devices in a mesh: groups: 2 (over x), gx: 16 (over z, y, core).
Axes of the slice: x: 2, y: 2, z: 4, core: 2. Of those that a mesh axis runs over, the one named last changes fastest.
Arguments:
- tokens: bfloat16 [768, 4608], P('groups', 'gx'), parts along dimension 0, may hold values from -6 to 6
- gate_weight: bfloat16 [16, 576, 9216], P('gx'), may hold values from -0.09375 to 0.09375
- up_weight: bfloat16 [16, 576, 9216], P('gx'), may hold values from -0.09375 to 0.09375
- down_weight: bfloat16 [16, 2304, 2304], P('gx'), may hold values from -0.046875 to 0.046875
Outputs:
- mixed: bfloat16 [768, 4608], P('groups', 'gx'), parts along dimension 0
There are 2 independent parts, one for each index of `groups`. A program takes and returns all parts, laid end to end along the dimension named above; an argument that names none is the same for every part. Nothing has to cross between parts.
All inputs are finite; a program needn't handle non-finite values.
Results may differ from a plain program's by a relative error of at most 0.015.
Values may be sent and summed in bfloat16 or wider, within the bound.
A program may use at most 128 MiB of HBM per device.

v0:
```python
import jax
import jax.numpy as jnp
from jax import lax
from jax.experimental import pallas as pl
from jax.experimental.pallas import tpu as pltpu
from jax.sharding import PartitionSpec as P

XS = 8
CHUNKS = 3
Z_PARTS, ALL_PARTS = 3, 8
VMEM_BYTES = 67043328
MESH = pl.DeviceIdType.MESH
DIAG, ZN, YN, OWN = 0, 1, 2, 3


def from_partner(block, axis, bit):
    count = lax.axis_size(axis)
    route = []
    for low in range(count):
        high = low | 1 << bit
        if high != low and high < count:
            route += [(low, high), (high, low)]
    return lax.ppermute(block, axis, route)


def bit_clear(device_index, bit_number):
    return device_index >> bit_number & 1 == 0


def plain_shards(tokens, gate_weight, up_weight, down_weight):
    gate_tile = gate_weight[0]
    up_tile = up_weight[0]
    down_tile = down_weight[0]
    axis_count = lax.axis_size("gx")
    column_groups = axis_count // XS
    low_bits = XS.bit_length() - 1
    high_bits = column_groups.bit_length() - 1
    device_index = lax.axis_index("gx")
    joined = tokens
    for high_step in range(high_bits):
        bit_number = low_bits + high_step
        partner_piece = from_partner(joined, "gx", bit_number)
        joined = jnp.where(
            bit_clear(device_index, bit_number),
            jnp.concatenate([joined, partner_piece], axis=1),
            jnp.concatenate([partner_piece, joined], axis=1),
        )
    gate_part = jnp.dot(joined, gate_tile, preferred_element_type=jnp.float32)
    up_part = jnp.dot(joined, up_tile, preferred_element_type=jnp.float32)
    stacked = jnp.stack([gate_part, up_part])
    for bit_number in range(low_bits - 1, -1, -1):
        half_width = stacked.shape[2] // 2
        lower_half = stacked[:, :, :half_width]
        upper_half = stacked[:, :, half_width:]
        keep_lower = bit_clear(device_index, bit_number)
        outgoing = jnp.where(keep_lower, upper_half, lower_half)
        kept_half = jnp.where(keep_lower, lower_half, upper_half)
        stacked = kept_half + from_partner(outgoing.astype(jnp.bfloat16), "gx", bit_number).astype(
            outgoing.dtype
        )
    hidden = (jax.nn.gelu(stacked[0], approximate=True) * stacked[1]).astype(jnp.bfloat16)
    hidden_joined = hidden
    for high_step in range(high_bits):
        bit_number = low_bits + high_step
        partner_hidden = from_partner(hidden_joined, "gx", bit_number)
        hidden_joined = jnp.where(
            bit_clear(device_index, bit_number),
            jnp.concatenate([hidden_joined, partner_hidden], axis=1),
            jnp.concatenate([partner_hidden, hidden_joined], axis=1),
        )
    partial_value = jnp.dot(hidden_joined, down_tile, preferred_element_type=jnp.float32)
    for bit_number in range(low_bits - 1, -1, -1):
        half_width = partial_value.shape[1] // 2
        lower_half = partial_value[:, :half_width]
        upper_half = partial_value[:, half_width:]
        keep_lower = bit_clear(device_index, bit_number)
        outgoing = jnp.where(keep_lower, upper_half, lower_half)
        kept_half = jnp.where(keep_lower, lower_half, upper_half)
        partial_value = kept_half + from_partner(
            outgoing.astype(jnp.bfloat16), "gx", bit_number
        ).astype(outgoing.dtype)
    return partial_value.astype(jnp.bfloat16)


def tile_of(width):
    for tiles in range(1, width // 128 + 1):
        if width % tiles == 0 and (width // tiles) % 128 == 0 and width // tiles <= 2304:
            return width // tiles
    return 128


def gelu(v):
    return 0.5 * v * (1.0 + jnp.tanh(0.7978845608 * (v + 0.044715 * (v * v * v))))


def kernel(
    tok, gate, up, down, out,
    tok_in, joined, wts, wd, sib_out, sib_in, z1_out, y1_out, z2_out, y2_out,
    z1_in, y1_in, z2_in, y2_in, keep_z, keep_y, keep_o, hid, hid_in,
    acc, blocks, keep_d, dsib_out, dsib_in, dout, din,
    tok_s, tok_r, w_sem, wd_sem, sib_s, sib_r, z1_s, z1_r, y1_s, y1_r,
    z2_s, z2_r, y2_s, y2_r, hid_s, hid_r, dsib_s, dsib_r, dout_s, dout_r,
):
    bf16, f32 = jnp.bfloat16, jnp.float32
    me = lax.axis_index("gx")
    c, yb, zb, a = me % 2, (me // 2) % 2, (me // 4) % 2, me // 8
    chunks = hid.shape[0]
    rows = hid.shape[1]
    feat = tok.shape[1]
    width = hid.shape[2]
    h0 = z1_out.shape[3]
    col = tile_of(width)
    ncol = width // col
    to_c = me + 1 - 2 * c
    to_y = me + 2 - 4 * yb
    to_z = me + 4 - 8 * zb
    to_d = me + 2 - 4 * yb + 4 - 8 * zb
    to_a = me + 8 - 16 * a

    def block_of(kind, core):
        zz = 1 - zb if kind in (DIAG, ZN) else zb
        yy = 1 - yb if kind in (DIAG, YN) else yb
        return zz * 4 + yy * 2 + core

    def remote(src, dst, ss, rs, target):
        return pltpu.make_async_remote_copy(
            src_ref=src, dst_ref=dst, send_sem=ss, recv_sem=rs,
            device_id={"gx": target}, device_id_type=MESH,
        )

    def weight_copies(slot):
        block = block_of(slot // 2, 1 - c if slot % 2 == 0 else c)
        cols = pl.ds(pl.multiple_of(block * width, 128), width)
        return [
            pltpu.make_async_copy(w.at[0, :, cols], wts.at[i, slot], w_sem.at[i, slot])
            for i, w in ((0, gate), (1, up))
        ]

    order = [2 * k for k in range(4)] + [2 * k + 1 for k in range(4)]
    for slot in order:
        for copy in weight_copies(slot):
            copy.start()
    down_copy = pltpu.make_async_copy(down.at[0], wd, wd_sem)
    down_copy.start()

    barrier = pltpu.get_barrier_semaphore()
    for target in (to_c, to_y, to_z, to_d, to_a):
        pl.semaphore_signal(barrier, inc=1, device_id={"gx": target}, device_id_type=MESH)
    pl.semaphore_wait(barrier, 5)

    def tok_copy(s):
        r = pl.ds(s * rows, rows)
        return remote(tok.at[r], tok_in.at[r], tok_s.at[s], tok_r.at[s], to_a)

    for s in range(chunks):
        tok_copy(s).start()

    def join(s):
        tok_copy(s).wait_recv()
        r = pl.ds(s * rows, rows)

        @pl.when(a == 0)
        def _():
            joined[r, 0:feat] = tok[r, :]
            joined[r, feat:2 * feat] = tok_in[r, :]

        @pl.when(a == 1)
        def _():
            joined[r, 0:feat] = tok_in[r, :]
            joined[r, feat:2 * feat] = tok[r, :]

    def each_tile(s, slot, body):
        if s == 0:
            for copy in weight_copies(slot):
                copy.wait()
        lhs = joined.at[pl.ds(s * rows, rows), :]

        def step(t, carry):
            g = t // ncol
            cols = pl.ds(pl.multiple_of((t % ncol) * col, 128), col)
            part = jnp.dot(lhs[...], wts[g, slot, :, cols], preferred_element_type=f32)
            body(g, cols, part)
            return carry

        lax.fori_loop(0, 2 * ncol, step, 0)

    def sib_copy(s, kind):
        return remote(sib_out.at[kind], sib_in.at[s, kind], sib_s.at[s, kind], sib_r.at[s, kind], to_c)

    def sibling(s, kind):
        if s > 0:
            sib_copy(s - 1, kind).wait_send()

        def body(g, cols, part):
            sib_out[kind, g, :, cols] = part.astype(bf16)

        each_tile(s, 2 * kind, body)
        sib_copy(s, kind).start()

    def z1_copy(s, piece):
        return remote(z1_out.at[s % 2, piece], z1_in.at[s, piece], z1_s.at[s, piece], z1_r.at[s, piece], to_z)

    def y1_copy(s, piece):
        return remote(y1_out.at[s % 2, piece], y1_in.at[s, piece], y1_s.at[s, piece], y1_r.at[s, piece], to_y)

    def z2_copy(s):
        return remote(z2_out.at[s % 2], z2_in.at[s], z2_s.at[s], z2_r.at[s], to_z)

    def y2_copy(s):
        return remote(y2_out.at[s % 2], y2_in.at[s], y2_s.at[s], y2_r.at[s], to_y)

    def own(s, kind):
        k = s % 2
        if s >= 2 and kind in (DIAG, ZN):
            z1_copy(s - 2, kind).wait_send()
        if s >= 2 and kind in (DIAG, YN):
            y1_copy(s - 2, 0 if kind == DIAG else 1).wait_send()
        sib_copy(s, kind).wait_recv()

        def body(g, cols, part):
            total = part + sib_in[s, kind, g, :, cols].astype(f32)
            if kind == DIAG:
                z1_out[k, 0, g, :, cols] = total[:h0].astype(bf16)
                y1_out[k, 0, g, :, cols] = total[h0:].astype(bf16)
            elif kind == ZN:
                z1_out[k, 1, g, :, cols] = total[:h0].astype(bf16)
                keep_z[k, g, :, cols] = total[h0:]
            elif kind == YN:
                y1_out[k, 1, g, :, cols] = total[h0:].astype(bf16)
                keep_y[k, g, :, cols] = total[:h0]
            else:
                keep_o[g, :, cols] = total

        each_tile(s, 2 * kind + 1, body)
        if kind == DIAG:
            z1_copy(s, 0).start()
            y1_copy(s, 0).start()
        elif kind == ZN:
            z1_copy(s, 1).start()
        elif kind == YN:
            y1_copy(s, 1).start()

    def loop_cols(body):
        def step(t, carry):
            body(t // ncol, pl.ds(pl.multiple_of((t % ncol) * col, 128), col))
            return carry

        lax.fori_loop(0, 2 * ncol, step, 0)

    def relay(s):
        k = s % 2
        if s >= 2:
            y2_copy(s - 2).wait_send()
            z2_copy(s - 2).wait_send()
        z1_copy(s, 0).wait_recv()

        def to_y2(g, cols):
            y2_out[k, g, :, cols] = (keep_y[k, g, :, cols] + z1_in[s, 0, g, :, cols].astype(f32)).astype(bf16)

        loop_cols(to_y2)
        y2_copy(s).start()
        y1_copy(s, 0).wait_recv()

        def to_z2(g, cols):
            z2_out[k, g, :, cols] = (keep_z[k, g, :, cols] + y1_in[s, 0, g, :, cols].astype(f32)).astype(bf16)

        loop_cols(to_z2)
        z2_copy(s).start()

    def hid_copy(s):
        return remote(hid.at[s], hid_in.at[s], hid_s.at[s], hid_r.at[s], to_a)

    def finish(s):
        own(s, OWN)
        z1_copy(s, 1).wait_recv()
        y1_copy(s, 1).wait_recv()
        y2_copy(s).wait_recv()
        z2_copy(s).wait_recv()

        def step(t, carry):
            cols = pl.ds(pl.multiple_of(t * col, 128), col)
            for r, first, second in (
                (slice(0, h0), z1_in.at[s, 1], y2_in.at[s]),
                (slice(h0, rows), y1_in.at[s, 1], z2_in.at[s]),
            ):
                g, u = (
                    keep_o[i, r, cols] + first[i, :, cols].astype(f32) + second[i, :, cols].astype(f32)
                    for i in (0, 1)
                )
                hid[s, r, cols] = (gelu(g) * u).astype(bf16)
            return carry

        lax.fori_loop(0, ncol, step, 0)
        hid_copy(s).start()

    full = acc.shape[1]
    dcol = tile_of(full)
    dwidth = blocks.shape[2]

    def dsib_copy(s, kind):
        return remote(dsib_out.at[s, kind], dsib_in.at[s, kind], dsib_s.at[s, kind], dsib_r.at[s, kind], to_c)

    def dout_copy(s, kind):
        target = (to_d, to_z, to_y)[kind]
        return remote(dout.at[s, kind], din.at[s, kind], dout_s.at[s, kind], dout_r.at[s, kind], target)

    def project(s):
        if s == 0:
            down_copy.wait()
        first = pl.ds(pl.multiple_of(a * width, 128), width)
        second = pl.ds(pl.multiple_of((1 - a) * width, 128), width)

        def own_half(t, carry):
            cols = pl.ds(pl.multiple_of(t * dcol, 128), dcol)
            acc[:, cols] = jnp.dot(hid[s], wd[first, cols], preferred_element_type=f32)
            return carry

        lax.fori_loop(0, full // dcol, own_half, 0)
        hid_copy(s).wait_recv()

        def other_half(t, carry):
            cols = pl.ds(pl.multiple_of(t * dcol, 128), dcol)
            acc[:, cols] += jnp.dot(hid_in[s], wd[second, cols], preferred_element_type=f32)
            return carry

        lax.fori_loop(0, full // dcol, other_half, 0)
        for b in range(XS):
            blocks[b] = acc[:, b * dwidth:(b + 1) * dwidth]
        for kind in range(4):
            dsib_out[s, kind] = blocks[block_of(kind, 1 - c)].astype(bf16)
            dsib_copy(s, kind).start()

    def spread(s):
        for kind in range(4):
            dsib_copy(s, kind).wait_recv()
            total = blocks[block_of(kind, c)] + dsib_in[s, kind].astype(f32)
            if kind == OWN:
                keep_d[s] = total
            else:
                dout[s, kind] = total.astype(bf16)
                dout_copy(s, kind).start()

    join(0)
    for kind in range(4):
        sibling(0, kind)
    for s in range(chunks):
        for kind in range(3):
            own(s, kind)
        if s + 1 < chunks:
            join(s + 1)
            for kind in range(4):
                sibling(s + 1, kind)
        if s > 0:
            finish(s - 1)
        relay(s)
    for s in range(chunks):
        if s < chunks - 1:
            project(s)
        if s == max(chunks - 2, 0):
            finish(chunks - 1)
        if s == chunks - 1:
            project(s)
        spread(s)
    for s in range(chunks):
        total = keep_d[s]
        for kind in range(3):
            dout_copy(s, kind).wait_recv()
            total = total + din[s, kind].astype(f32)
        out[pl.ds(s * rows, rows), :] = total.astype(bf16)

    for s in range(chunks):
        tok_copy(s).wait_send()
        hid_copy(s).wait_send()
        for kind in range(4):
            if s == chunks - 1:
                sib_copy(s, kind).wait_send()
            dsib_copy(s, kind).wait_send()
        for kind in range(3):
            dout_copy(s, kind).wait_send()
        if s >= chunks - 2:
            for piece in range(2):
                z1_copy(s, piece).wait_send()
                y1_copy(s, piece).wait_send()
            z2_copy(s).wait_send()
            y2_copy(s).wait_send()


def fused(chunks, tokens, gate_weight, up_weight, down_weight):
    count, feat = tokens.shape
    depth, half = gate_weight.shape[1:]
    deep, full = down_weight.shape[1:]
    rows, width, dwidth = count // chunks, half // XS, full // XS
    h0 = rows // 16 * Z_PARTS // ALL_PARTS * 16
    h1 = rows - h0
    bf16, f32 = jnp.bfloat16, jnp.float32
    v = pltpu.VMEM
    pair = min(chunks, 2)
    buffers = [
        v((count, feat), bf16),
        v((count, 2 * feat), bf16),
        v((2, XS, depth, width), bf16),
        v((deep, full), bf16),
        v((4, 2, rows, width), bf16),
        v((chunks, 4, 2, rows, width), bf16),
        v((pair, 2, 2, h0, width), bf16),
        v((pair, 2, 2, h1, width), bf16),
        v((pair, 2, h1, width), bf16),
        v((pair, 2, h0, width), bf16),
        v((chunks, 2, 2, h0, width), bf16),
        v((chunks, 2, 2, h1, width), bf16),
        v((chunks, 2, h1, width), bf16),
        v((chunks, 2, h0, width), bf16),
        v((pair, 2, h1, width), f32),
        v((pair, 2, h0, width), f32),
        v((2, rows, width), f32),
        v((chunks, rows, width), bf16),
        v((chunks, rows, width), bf16),
        v((rows, full), f32),
        v((XS, rows, dwidth), f32),
        v((chunks, rows, dwidth), f32),
        v((chunks, 4, rows, dwidth), bf16),
        v((chunks, 4, rows, dwidth), bf16),
        v((chunks, 3, rows, dwidth), bf16),
        v((chunks, 3, rows, dwidth), bf16),
    ]
    sem = pltpu.SemaphoreType.DMA
    s = chunks
    shapes = [(s,), (s,), (2, XS), None, (s, 4), (s, 4), (s, 2), (s, 2), (s, 2), (s, 2)]
    shapes += [(s,)] * 6 + [(s, 4), (s, 4), (s, 3), (s, 3)]
    sems = [sem if shape is None else sem(shape) for shape in shapes]
    vmem = pl.BlockSpec(memory_space=pltpu.VMEM)
    hbm = pl.BlockSpec(memory_space=pl.ANY)
    return pl.pallas_call(
        kernel,
        out_shape=jax.ShapeDtypeStruct((count, dwidth), bf16),
        in_specs=[vmem, hbm, hbm, hbm],
        out_specs=vmem,
        scratch_shapes=buffers + sems,
        compiler_params=pltpu.CompilerParams(
            collective_id=0, has_side_effects=True, vmem_limit_bytes=VMEM_BYTES
        ),
    )(tokens, gate_weight, up_weight, down_weight)


def shards(tokens, gate_weight, up_weight, down_weight):
    width = gate_weight.shape[2] // XS
    suits = (
        lax.axis_size("gx") == 2 * XS
        and width % 128 == 0
        and down_weight.shape[2] % 128 == 0
        and tokens.shape[0] % (CHUNKS * 64) == 0
        and tokens.shape[1] % 16 == 0
    )
    if suits:
        return fused(CHUNKS, tokens, gate_weight, up_weight, down_weight)
    return plain_shards(tokens, gate_weight, up_weight, down_weight)


def solution(mesh):
    placed = (P("groups", "gx"), P("gx", None, None), P("gx", None, None), P("gx", None, None))
    return jax.shard_map(
        shards, mesh=mesh, in_specs=placed, out_specs=P("groups", "gx"), check_vma=False
    )
```

profile of v0, /device:TPU:0, one launch (start us, length us, event | category | flops | bytes accessed | tf_op | source)
XLA Modules:
  0.0 113.0 jit_solution(3607257849968028829)
XLA Ops:
  0.0 1.8 %copy.5.tok = bf16[384,288]{1,0:T(8,128)(2,1)} copy(bf16[384,288]{0,1:T(8,128)(2,1)} %param.4) | data formatting | bytes 442368 | tf_op args[0]
  1.8 109.4 %shard_map.46 = bf16[384,288]{1,0:T(8,128)(2,1)} custom-call(bf16[384,288]{1,0:T(8,128)(2,1)} %copy.5.tok, bf16[1,576,9216]{2,1,0:T(8,128)(2,1)} %gate.1, bf16[1,576,9216]{2,1,0:T(8,128)(2,1)} %up.1, bf16[1,2304,2304]{2,1,0:T(8,128)(2,1)} %down.1), custom_call_target="tpu_custom_call" | custom-call | tf_op jit(solution)/shard_map/pallas_call | solution.py:433
  111.2 1.8 %copy.6 = bf16[384,288]{0,1:T(8,128)(2,1)} copy(bf16[384,288]{1,0:T(8,128)(2,1)} %shard_map.46) | data formatting | bytes 442368 | tf_op jit(solution)/shard_map/pallas_call | solution.py:433
where the time goes:
time: 113 us
  Pallas kernels  109 us (96%)
  local copies, waits for them, and re-layouts  3.61 us (3%)
    pallas_call x1, Pallas kernels, fused(): pl.pallas_call(kernel, out_shape=jax.ShapeDtypeStruct((count, dwidth), bf...  109 us

commit v1 on v0

v1 whole, which is shorter than its diff:
```python
import functools

import jax
import jax.numpy as jnp
from jax import lax
from jax.experimental import pallas as pl
from jax.experimental.pallas import tpu as pltpu
from jax.sharding import PartitionSpec as P

XS = 8
PLAN = (2, 4, 3, 2, 1)
Z_ROWS = (1, 3, 2, 1, 1)
VMEM_BYTES = 67043328
MESH = pl.DeviceIdType.MESH
DIAG, ZN, YN, OWN = 0, 1, 2, 3


def from_partner(block, axis, bit):
    count = lax.axis_size(axis)
    route = []
    for low in range(count):
        high = low | 1 << bit
        if high != low and high < count:
            route += [(low, high), (high, low)]
    return lax.ppermute(block, axis, route)


def bit_clear(device_index, bit_number):
    return device_index >> bit_number & 1 == 0


def plain_shards(tokens, gate_weight, up_weight, down_weight):
    gate_tile = gate_weight[0]
    up_tile = up_weight[0]
    down_tile = down_weight[0]
    axis_count = lax.axis_size("gx")
    column_groups = axis_count // XS
    low_bits = XS.bit_length() - 1
    high_bits = column_groups.bit_length() - 1
    device_index = lax.axis_index("gx")
    joined = tokens
    for high_step in range(high_bits):
        bit_number = low_bits + high_step
        partner_piece = from_partner(joined, "gx", bit_number)
        joined = jnp.where(
            bit_clear(device_index, bit_number),
            jnp.concatenate([joined, partner_piece], axis=1),
            jnp.concatenate([partner_piece, joined], axis=1),
        )
    gate_part = jnp.dot(joined, gate_tile, preferred_element_type=jnp.float32)
    up_part = jnp.dot(joined, up_tile, preferred_element_type=jnp.float32)
    stacked = jnp.stack([gate_part, up_part])
    for bit_number in range(low_bits - 1, -1, -1):
        half_width = stacked.shape[2] // 2
        lower_half = stacked[:, :, :half_width]
        upper_half = stacked[:, :, half_width:]
        keep_lower = bit_clear(device_index, bit_number)
        outgoing = jnp.where(keep_lower, upper_half, lower_half)
        kept_half = jnp.where(keep_lower, lower_half, upper_half)
        stacked = kept_half + from_partner(outgoing.astype(jnp.bfloat16), "gx", bit_number).astype(
            outgoing.dtype
        )
    hidden = (jax.nn.gelu(stacked[0], approximate=True) * stacked[1]).astype(jnp.bfloat16)
    hidden_joined = hidden
    for high_step in range(high_bits):
        bit_number = low_bits + high_step
        partner_hidden = from_partner(hidden_joined, "gx", bit_number)
        hidden_joined = jnp.where(
            bit_clear(device_index, bit_number),
            jnp.concatenate([hidden_joined, partner_hidden], axis=1),
            jnp.concatenate([partner_hidden, hidden_joined], axis=1),
        )
    partial_value = jnp.dot(hidden_joined, down_tile, preferred_element_type=jnp.float32)
    for bit_number in range(low_bits - 1, -1, -1):
        half_width = partial_value.shape[1] // 2
        lower_half = partial_value[:, :half_width]
        upper_half = partial_value[:, half_width:]
        keep_lower = bit_clear(device_index, bit_number)
        outgoing = jnp.where(keep_lower, upper_half, lower_half)
        kept_half = jnp.where(keep_lower, lower_half, upper_half)
        partial_value = kept_half + from_partner(
            outgoing.astype(jnp.bfloat16), "gx", bit_number
        ).astype(outgoing.dtype)
    return partial_value.astype(jnp.bfloat16)


def tile_of(width):
    for tiles in range(1, width // 128 + 1):
        if width % tiles == 0 and (width // tiles) % 128 == 0 and width // tiles <= 2304:
            return width // tiles
    return 128


def gelu(v):
    return 0.5 * v * (1.0 + jnp.tanh(0.7978845608 * (v + 0.044715 * (v * v * v))))


def kernel(
    plan, halves, tok_t, gate, up, down, out_t,
    raw, tok, tok_in, joined, wts, wd, sib_out, sib_in, z1_out, y1_out, z2_out, y2_out,
    z1_in, y1_in, z2_in, y2_in, keep_z, keep_y, keep_o, hid, hid_in,
    acc, blocks, keep_d, dsib_out, dsib_in, dout, din, done,
    raw_sem, tok_s, tok_r, w_sem, wd_sem, sib_s, sib_r, z1_s, z1_r, y1_s, y1_r,
    z2_s, z2_r, y2_s, y2_r, hid_s, hid_r, dsib_s, dsib_r, dout_s, dout_r, out_sem,
):
    bf16, f32 = jnp.bfloat16, jnp.float32
    me = lax.axis_index("gx")
    c, yb, zb, a = me % 2, (me // 2) % 2, (me // 4) % 2, me // 8
    chunks = len(plan)
    starts = [sum(plan[:s]) for s in range(chunks)]
    others = [rows - z for rows, z in zip(plan, halves)]
    z_starts = [sum(halves[:s]) for s in range(chunks)]
    y_starts = [sum(others[:s]) for s in range(chunks)]
    feat, count = raw.shape
    width = hid.shape[1]
    col = tile_of(width)
    ncol = width // col
    to_c = me + 1 - 2 * c
    to_y = me + 2 - 4 * yb
    to_z = me + 4 - 8 * zb
    to_d = me + 2 - 4 * yb + 4 - 8 * zb
    to_a = me + 8 - 16 * a

    def span(s):
        return pl.ds(starts[s], plan[s])

    def z_span(s):
        return pl.ds(z_starts[s], halves[s])

    def y_span(s):
        return pl.ds(y_starts[s], others[s])

    def block_of(kind, core):
        zz = 1 - zb if kind in (DIAG, ZN) else zb
        yy = 1 - yb if kind in (DIAG, YN) else yb
        return zz * 4 + yy * 2 + core

    def remote(src, dst, ss, rs, target):
        return pltpu.make_async_remote_copy(
            src_ref=src, dst_ref=dst, send_sem=ss, recv_sem=rs,
            device_id={"gx": target}, device_id_type=MESH,
        )

    def weight_copies(slot):
        block = block_of(slot // 2, 1 - c if slot % 2 == 0 else c)
        cols = pl.ds(pl.multiple_of(block * width, 128), width)
        return [
            pltpu.make_async_copy(w.at[0, :, cols], wts.at[i, slot], w_sem.at[i, slot])
            for i, w in ((0, gate), (1, up))
        ]

    raw_copy = pltpu.make_async_copy(tok_t, raw, raw_sem)
    raw_copy.start()
    barrier = pltpu.get_barrier_semaphore()
    for target in (to_a, to_d, to_z, to_y, to_c):
        pl.semaphore_signal(barrier, inc=1, device_id={"gx": target}, device_id_type=MESH)
    order = [0, 2, 4, 1, 6, 3, 5, 7]
    for slot in order:
        for copy in weight_copies(slot):
            copy.start()
    down_copy = pltpu.make_async_copy(down.at[0], wd, wd_sem)
    down_copy.start()
    raw_copy.wait()
    for first in range(0, count, 128):
        tok[first:first + 128, :] = raw[:, first:first + 128].T
    pl.semaphore_wait(barrier, 5)

    def tok_copy(s):
        r = span(s)
        return remote(tok.at[r], tok_in.at[r], tok_s.at[s], tok_r.at[s], to_a)

    def join(s):
        tok_copy(s).wait_recv()
        if s + 1 < chunks:
            tok_copy(s + 1).start()
        r = span(s)

        @pl.when(a == 0)
        def _():
            joined[r, 0:feat] = tok[r, :]
            joined[r, feat:2 * feat] = tok_in[r, :]

        @pl.when(a == 1)
        def _():
            joined[r, 0:feat] = tok_in[r, :]
            joined[r, feat:2 * feat] = tok[r, :]

    def each_tile(s, slot, body):
        if s == 0:
            for copy in weight_copies(slot):
                copy.wait()
        lhs = joined.at[span(s), :]

        def step(t, carry):
            g = t // ncol
            cols = pl.ds(pl.multiple_of((t % ncol) * col, 128), col)
            part = jnp.dot(lhs[...], wts[g, slot, :, cols], preferred_element_type=f32)
            body(g, cols, part)
            return carry

        lax.fori_loop(0, 2 * ncol, step, 0)

    def sib_copy(s, kind):
        return remote(
            sib_out.at[kind, :, pl.ds(0, plan[s])], sib_in.at[kind, :, span(s)],
            sib_s.at[s, kind], sib_r.at[s, kind], to_c,
        )

    def sibling(s, kind):
        if s > 0:
            sib_copy(s - 1, kind).wait_send()

        def body(g, cols, part):
            sib_out[kind, g, 0:plan[s], cols] = part.astype(bf16)

        each_tile(s, 2 * kind, body)
        sib_copy(s, kind).start()

    def z1_copy(s, piece):
        return remote(
            z1_out.at[s % 2, piece, :, pl.ds(0, halves[s])], z1_in.at[piece, :, z_span(s)],
            z1_s.at[s, piece], z1_r.at[s, piece], to_z,
        )

    def y1_copy(s, piece):
        return remote(
            y1_out.at[s % 2, piece, :, pl.ds(0, others[s])], y1_in.at[piece, :, y_span(s)],
            y1_s.at[s, piece], y1_r.at[s, piece], to_y,
        )

    def z2_copy(s):
        return remote(
            z2_out.at[s % 2, :, pl.ds(0, others[s])], z2_in.at[:, y_span(s)], z2_s.at[s], z2_r.at[s], to_z
        )

    def y2_copy(s):
        return remote(
            y2_out.at[s % 2, :, pl.ds(0, halves[s])], y2_in.at[:, z_span(s)], y2_s.at[s], y2_r.at[s], to_y
        )

    def own(s, kind):
        k = s % 2
        h0, h1 = halves[s], others[s]
        if s >= 2 and kind in (DIAG, ZN):
            z1_copy(s - 2, kind).wait_send()
        if s >= 2 and kind in (DIAG, YN):
            y1_copy(s - 2, 0 if kind == DIAG else 1).wait_send()
        sib_copy(s, kind).wait_recv()

        def body(g, cols, part):
            total = part + sib_in[kind, g, span(s), cols].astype(f32)
            if kind == DIAG:
                z1_out[k, 0, g, 0:h0, cols] = total[:h0].astype(bf16)
                y1_out[k, 0, g, 0:h1, cols] = total[h0:].astype(bf16)
            elif kind == ZN:
                z1_out[k, 1, g, 0:h0, cols] = total[:h0].astype(bf16)
                keep_z[k, g, 0:h1, cols] = total[h0:]
            elif kind == YN:
                y1_out[k, 1, g, 0:h1, cols] = total[h0:].astype(bf16)
                keep_y[k, g, 0:h0, cols] = total[:h0]
            else:
                keep_o[g, 0:h0 + h1, cols] = total

        each_tile(s, 2 * kind + 1, body)
        if kind == DIAG:
            z1_copy(s, 0).start()
            y1_copy(s, 0).start()
        elif kind == ZN:
            z1_copy(s, 1).start()
        elif kind == YN:
            y1_copy(s, 1).start()

    def loop_cols(body):
        def step(t, carry):
            body(t // ncol, pl.ds(pl.multiple_of((t % ncol) * col, 128), col))
            return carry

        lax.fori_loop(0, 2 * ncol, step, 0)

    def relay(s):
        k = s % 2
        h0, h1 = halves[s], others[s]
        if s >= 2:
            y2_copy(s - 2).wait_send()
            z2_copy(s - 2).wait_send()
        z1_copy(s, 0).wait_recv()

        def to_y2(g, cols):
            total = keep_y[k, g, 0:h0, cols] + z1_in[0, g, z_span(s), cols].astype(f32)
            y2_out[k, g, 0:h0, cols] = total.astype(bf16)

        loop_cols(to_y2)
        y2_copy(s).start()
        y1_copy(s, 0).wait_recv()

        def to_z2(g, cols):
            total = keep_z[k, g, 0:h1, cols] + y1_in[0, g, y_span(s), cols].astype(f32)
            z2_out[k, g, 0:h1, cols] = total.astype(bf16)

        loop_cols(to_z2)
        z2_copy(s).start()

    def hid_copy(s):
        r = span(s)
        return remote(hid.at[r], hid_in.at[r], hid_s.at[s], hid_r.at[s], to_a)

    def finish(s):
        own(s, OWN)
        z1_copy(s, 1).wait_recv()
        y1_copy(s, 1).wait_recv()
        y2_copy(s).wait_recv()
        z2_copy(s).wait_recv()
        h0, rows = halves[s], plan[s]

        def step(t, carry):
            cols = pl.ds(pl.multiple_of(t * col, 128), col)
            for low, high, first, second in (
                (0, h0, z1_in.at[1, :, z_span(s)], y2_in.at[:, z_span(s)]),
                (h0, rows, y1_in.at[1, :, y_span(s)], z2_in.at[:, y_span(s)]),
            ):
                g, u = (
                    keep_o[i, low:high, cols] + first[i, :, cols].astype(f32) + second[i, :, cols].astype(f32)
                    for i in (0, 1)
                )
                hid[pl.ds(starts[s] + low, high - low), cols] = (gelu(g) * u).astype(bf16)
            return carry

        lax.fori_loop(0, ncol, step, 0)
        hid_copy(s).start()

    full = acc.shape[1]
    dcol = tile_of(full)
    dwidth = blocks.shape[2]

    def dsib_copy(s, kind):
        r = span(s)
        return remote(
            dsib_out.at[kind, r], dsib_in.at[kind, r], dsib_s.at[s, kind], dsib_r.at[s, kind], to_c
        )

    def dout_copy(s, kind):
        r = span(s)
        target = (to_d, to_z, to_y)[kind]
        return remote(dout.at[kind, r], din.at[kind, r], dout_s.at[s, kind], dout_r.at[s, kind], target)

    def project(s):
        rows = plan[s]
        if s == 0:
            down_copy.wait()
        first = pl.ds(pl.multiple_of(a * width, 128), width)
        second = pl.ds(pl.multiple_of((1 - a) * width, 128), width)
        mine, theirs = hid.at[span(s), :], hid_in.at[span(s), :]

        def own_half(t, carry):
            cols = pl.ds(pl.multiple_of(t * dcol, 128), dcol)
            acc[0:rows, cols] = jnp.dot(mine[...], wd[first, cols], preferred_element_type=f32)
            return carry

        lax.fori_loop(0, full // dcol, own_half, 0)
        hid_copy(s).wait_recv()

        def other_half(t, carry):
            cols = pl.ds(pl.multiple_of(t * dcol, 128), dcol)
            acc[0:rows, cols] += jnp.dot(theirs[...], wd[second, cols], preferred_element_type=f32)
            return carry

        lax.fori_loop(0, full // dcol, other_half, 0)
        for b in range(XS):
            blocks[b, 0:rows] = acc[0:rows, b * dwidth:(b + 1) * dwidth]
        for kind in range(4):
            dsib_out[kind, span(s)] = blocks[block_of(kind, 1 - c), 0:rows].astype(bf16)
            dsib_copy(s, kind).start()

    def spread(s):
        for kind in range(4):
            dsib_copy(s, kind).wait_recv()
            total = blocks[block_of(kind, c), 0:plan[s]] + dsib_in[kind, span(s)].astype(f32)
            if kind == OWN:
                keep_d[span(s)] = total
            else:
                dout[kind, span(s)] = total.astype(bf16)

    def send_out(s):
        for kind in range(3):
            dout_copy(s, kind).start()

    def collect(s):
        total = keep_d[span(s)]
        for kind in range(3):
            dout_copy(s, kind).wait_recv()
            total = total + din[kind, span(s)].astype(f32)
        keep_d[span(s)] = total

    last = chunks - 1
    tok_copy(0).start()
    join(0)
    for kind in (DIAG, ZN, YN):
        sibling(0, kind)
    own(0, DIAG)
    sibling(0, OWN)
    own(0, ZN)
    own(0, YN)
    projected = 0
    for s in range(chunks):
        if s > 0:
            for kind in range(3):
                own(s, kind)
        if s < last:
            join(s + 1)
            for kind in range(4):
                sibling(s + 1, kind)
        if s >= 3:
            project(projected)
        if s > 0:
            finish(s - 1)
        if s >= 3:
            spread(projected)
            projected += 1
        relay(s)
    for s in range(projected):
        send_out(s)
    while projected < last:
        project(projected)
        if projected == last - 2 or last < 2:
            finish(last)
        spread(projected)
        send_out(projected)
        projected += 1
    project(last)
    spread(last)
    send_out(last)
    for s in range(chunks):
        collect(s)
    for first in range(0, count, 128):
        done[:, first:first + 128] = keep_d[first:first + 128, :].T.astype(bf16)
    out_copy = pltpu.make_async_copy(done, out_t, out_sem)
    out_copy.start()

    for s in range(chunks):
        tok_copy(s).wait_send()
        hid_copy(s).wait_send()
        for kind in range(4):
            if s == last:
                sib_copy(s, kind).wait_send()
            dsib_copy(s, kind).wait_send()
        for kind in range(3):
            dout_copy(s, kind).wait_send()
        if s >= chunks - 2:
            for piece in range(2):
                z1_copy(s, piece).wait_send()
                y1_copy(s, piece).wait_send()
            z2_copy(s).wait_send()
            y2_copy(s).wait_send()
    out_copy.wait()


def plan_of(count):
    unit = count // sum(PLAN)
    plan = [unit * parts for parts in PLAN]
    halves = [unit // 2 * parts for parts in Z_ROWS]
    return plan, halves


def fused(tokens, gate_weight, up_weight, down_weight):
    count, feat = tokens.shape
    depth, half = gate_weight.shape[1:]
    deep, full = down_weight.shape[1:]
    width, dwidth = half // XS, full // XS
    plan, halves = plan_of(count)
    others = [rows - z for rows, z in zip(plan, halves)]
    rows, h0, h1 = max(plan), max(halves), max(others)
    all0, all1 = sum(halves), sum(others)
    bf16, f32 = jnp.bfloat16, jnp.float32
    v = pltpu.VMEM
    buffers = [
        v((feat, count), bf16),
        v((count, feat), bf16),
        v((count, feat), bf16),
        v((count, 2 * feat), bf16),
        v((2, XS, depth, width), bf16),
        v((deep, full), bf16),
        v((4, 2, rows, width), bf16),
        v((4, 2, count, width), bf16),
        v((2, 2, 2, h0, width), bf16),
        v((2, 2, 2, h1, width), bf16),
        v((2, 2, h1, width), bf16),
        v((2, 2, h0, width), bf16),
        v((2, 2, all0, width), bf16),
        v((2, 2, all1, width), bf16),
        v((2, all1, width), bf16),
        v((2, all0, width), bf16),
        v((2, 2, h1, width), f32),
        v((2, 2, h0, width), f32),
        v((2, rows, width), f32),
        v((count, width), bf16),
        v((count, width), bf16),
        v((rows, full), f32),
        v((XS, rows, dwidth), f32),
        v((count, dwidth), f32),
        v((4, count, dwidth), bf16),
        v((4, count, dwidth), bf16),
        v((3, count, dwidth), bf16),
        v((3, count, dwidth), bf16),
        v((dwidth, count), bf16),
    ]
    sem = pltpu.SemaphoreType.DMA
    s = len(plan)
    shapes = [None, (s,), (s,), (2, XS), None, (s, 4), (s, 4), (s, 2), (s, 2), (s, 2), (s, 2)]
    shapes += [(s,)] * 6 + [(s, 4), (s, 4), (s, 3), (s, 3), None]
    sems = [sem if shape is None else sem(shape) for shape in shapes]
    hbm = pl.BlockSpec(memory_space=pl.ANY)
    result = pl.pallas_call(
        functools.partial(kernel, plan, halves),
        out_shape=jax.ShapeDtypeStruct((dwidth, count), bf16),
        in_specs=[hbm, hbm, hbm, hbm],
        out_specs=hbm,
        scratch_shapes=buffers + sems,
        compiler_params=pltpu.CompilerParams(
            collective_id=0, has_side_effects=True, vmem_limit_bytes=VMEM_BYTES
        ),
    )(tokens.T, gate_weight, up_weight, down_weight)
    return result.T


def shards(tokens, gate_weight, up_weight, down_weight):
    width = gate_weight.shape[2] // XS
    suits = (
        lax.axis_size("gx") == 2 * XS
        and width % 128 == 0
        and down_weight.shape[2] % 128 == 0
        and tokens.shape[0] % (32 * sum(PLAN)) == 0
        and tokens.shape[0] % 128 == 0
        and tokens.shape[1] % 16 == 0
        and tokens.shape[1] == down_weight.shape[2] // XS
    )
    if suits:
        return fused(tokens, gate_weight, up_weight, down_weight)
    return plain_shards(tokens, gate_weight, up_weight, down_weight)


def solution(mesh):
    placed = (P("groups", "gx"), P("gx", None, None), P("gx", None, None), P("gx", None, None))
    return jax.shard_map(
        shards, mesh=mesh, in_specs=placed, out_specs=P("groups", "gx"), check_vma=False
    )
```

time: 113 us -> 106 us (0.938)
  Pallas kernels: 109 us -> 104 us
  local copies, waits for them, and re-layouts: 3.61 us -> 1.64 us
    pallas_call x1, Pallas kernels: 109 us -> 104 us  [fused(): pl.pallas_call(functools.partial(kernel, plan, halves), out_shape=jax.Sha...]
    pallas_call x1 -> x0, local copies, waits for them, and re-layouts: 1.79 us -> none  [fused(): pl.pallas_call(kernel, out_shape=jax.ShapeDtypeStruct((count, dwidth), bf...]
where the time goes in v1:
time: 106 us; the launch traced here: 105 us
  Pallas kernels  104 us (98%)
  local copies, waits for them, and re-layouts  1.64 us (2%)
    pallas_call x1, Pallas kernels, fused(): pl.pallas_call(functools.partial(kernel, plan, halves), out_shape=jax.Sha...  104 us

profile of v1, /device:TPU:0, one launch (start us, length us, event | category | flops | bytes accessed | tf_op | source)
XLA Modules:
  0.0 105.5 jit_solution(7835841655316440047)
XLA Ops:
  0.0 103.8 %shard_map.46 = bf16[288,384]{1,0:T(8,128)(2,1)} custom-call(bf16[288,384]{1,0:T(8,128)(2,1)} %bitcast.3, bf16[1,576,9216]{2,1,0:T(8,128)(2,1)} %gate.1, bf16[1,576,9216]{2,1,0:T(8,128)(2,1)} %up.1, bf16[1,2304,2304]{2,1,0:T(8,128)(2,1)} %down.1), custom_call_target="tpu_custom_call" | custom-call | tf_op jit(solution)/shard_map/pallas_call | solution.py:512
  103.8 1.6 %copy.6 = bf16[384,288]{0,1:T(8,128)(2,1)} copy(bf16[384,288]{0,1:T(8,128)(2,1)} %bitcast.2) | data formatting | bytes 442368

commit v2 on v1

--- a/solution.py
+++ b/solution.py
@@ -8,8 +8,10 @@
 from jax.sharding import PartitionSpec as P
 
 XS = 8
-PLAN = (2, 4, 3, 2, 1)
-Z_ROWS = (1, 3, 2, 1, 1)
+PLAN = (4, 7, 6, 5, 2)
+Z_ROWS = (2, 2, 2, 1, 0)
+RELAYED = 3
+Z_FIRST = True
 VMEM_BYTES = 67043328
 MESH = pl.DeviceIdType.MESH
 DIAG, ZN, YN, OWN = 0, 1, 2, 3
@@ -99,7 +101,7 @@
     plan, halves, tok_t, gate, up, down, out_t,
     raw, tok, tok_in, joined, wts, wd, sib_out, sib_in, z1_out, y1_out, z2_out, y2_out,
     z1_in, y1_in, z2_in, y2_in, keep_z, keep_y, keep_o, hid, hid_in,
-    acc, blocks, keep_d, dsib_out, dsib_in, dout, din, done,
+    acc, blocks, keep_d, keep_n, dsib_out, dsib_in, dout, din, done,
     raw_sem, tok_s, tok_r, w_sem, wd_sem, sib_s, sib_r, z1_s, z1_r, y1_s, y1_r,
     z2_s, z2_r, y2_s, y2_r, hid_s, hid_r, dsib_s, dsib_r, dout_s, dout_r, out_sem,
 ):
@@ -107,6 +109,7 @@
     me = lax.axis_index("gx")
     c, yb, zb, a = me % 2, (me // 2) % 2, (me // 4) % 2, me // 8
     chunks = len(plan)
+    last = chunks - 1
     starts = [sum(plan[:s]) for s in range(chunks)]
     others = [rows - z for rows, z in zip(plan, halves)]
     z_starts = [sum(halves[:s]) for s in range(chunks)]
@@ -145,7 +148,7 @@
         block = block_of(slot // 2, 1 - c if slot % 2 == 0 else c)
         cols = pl.ds(pl.multiple_of(block * width, 128), width)
         return [
-            pltpu.make_async_copy(w.at[0, :, cols], wts.at[i, slot], w_sem.at[i, slot])
+            pltpu.make_async_copy(w.at[0, :, cols], wts.at[i, slot], w_sem.at[slot])
             for i, w in ((0, gate), (1, up))
         ]
 
@@ -167,7 +170,7 @@
 
     def tok_copy(s):
         r = span(s)
-        return remote(tok.at[r], tok_in.at[r], tok_s.at[s], tok_r.at[s], to_a)
+        return remote(tok.at[r], tok_in.at[r], tok_s, tok_r.at[s], to_a)
 
     def join(s):
         tok_copy(s).wait_recv()
@@ -187,8 +190,8 @@
 
     def each_tile(s, slot, body):
         if s == 0:
-            for copy in weight_copies(slot):
-                copy.wait()
+            both = wts.at[:, slot]
+            pltpu.make_async_copy(both, both, w_sem.at[slot]).wait()
         lhs = joined.at[span(s), :]
 
         def step(t, carry):
@@ -201,72 +204,82 @@
         lax.fori_loop(0, 2 * ncol, step, 0)
 
     def sib_copy(s, kind):
+        if s == 0:
+            return remote(
+                sib_out.at[kind, :, pl.ds(0, plan[s])], sib_in.at[kind, :, span(s)],
+                sib_s.at[kind], sib_r.at[kind], to_c,
+            )
         return remote(
-            sib_out.at[kind, :, pl.ds(0, plan[s])], sib_in.at[kind, :, span(s)],
-            sib_s.at[s, kind], sib_r.at[s, kind], to_c,
+            sib_out.at[:, :, pl.ds(0, plan[s])], sib_in.at[:, :, span(s)], sib_s.at[4], sib_r.at[3 + s], to_c
         )
 
     def sibling(s, kind):
-        if s > 0:
+        if s == 1:
+            sib_copy(0, kind).wait_send()
+        elif s > 1 and kind == 0:
             sib_copy(s - 1, kind).wait_send()
 
         def body(g, cols, part):
             sib_out[kind, g, 0:plan[s], cols] = part.astype(bf16)
 
         each_tile(s, 2 * kind, body)
-        sib_copy(s, kind).start()
+        if s == 0 or kind == 3:
+            sib_copy(s, kind).start()
 
     def z1_copy(s, piece):
         return remote(
             z1_out.at[s % 2, piece, :, pl.ds(0, halves[s])], z1_in.at[piece, :, z_span(s)],
-            z1_s.at[s, piece], z1_r.at[s, piece], to_z,
+            z1_s.at[s % 2, piece], z1_r.at[s, piece], to_z,
         )
 
     def y1_copy(s, piece):
         return remote(
             y1_out.at[s % 2, piece, :, pl.ds(0, others[s])], y1_in.at[piece, :, y_span(s)],
-            y1_s.at[s, piece], y1_r.at[s, piece], to_y,
+            y1_s.at[s % 2, piece], y1_r.at[s, piece], to_y,
         )
 
     def z2_copy(s):
         return remote(
-            z2_out.at[s % 2, :, pl.ds(0, others[s])], z2_in.at[:, y_span(s)], z2_s.at[s], z2_r.at[s], to_z
+            z2_out.at[s % 2, :, pl.ds(0, others[s])], z2_in.at[:, y_span(s)], z2_s.at[s % 2], z2_r.at[s], to_z
         )
 
     def y2_copy(s):
         return remote(
-            y2_out.at[s % 2, :, pl.ds(0, halves[s])], y2_in.at[:, z_span(s)], y2_s.at[s], y2_r.at[s], to_y
+            y2_out.at[s % 2, :, pl.ds(0, halves[s])], y2_in.at[:, z_span(s)], y2_s.at[s % 2], y2_r.at[s], to_y
         )
 
     def own(s, kind):
         k = s % 2
         h0, h1 = halves[s], others[s]
-        if s >= 2 and kind in (DIAG, ZN):
+        if s >= 2 and kind in (DIAG, ZN) and halves[s - 2]:
             z1_copy(s - 2, kind).wait_send()
         if s >= 2 and kind in (DIAG, YN):
             y1_copy(s - 2, 0 if kind == DIAG else 1).wait_send()
-        sib_copy(s, kind).wait_recv()
+        if s == 0 or kind == 0:
+            sib_copy(s, kind).wait_recv()
 
         def body(g, cols, part):
             total = part + sib_in[kind, g, span(s), cols].astype(f32)
             if kind == DIAG:
-                z1_out[k, 0, g, 0:h0, cols] = total[:h0].astype(bf16)
+                if h0:
+                    z1_out[k, 0, g, 0:h0, cols] = total[:h0].astype(bf16)
                 y1_out[k, 0, g, 0:h1, cols] = total[h0:].astype(bf16)
             elif kind == ZN:
-                z1_out[k, 1, g, 0:h0, cols] = total[:h0].astype(bf16)
+                if h0:
+                    z1_out[k, 1, g, 0:h0, cols] = total[:h0].astype(bf16)
                 keep_z[k, g, 0:h1, cols] = total[h0:]
             elif kind == YN:
                 y1_out[k, 1, g, 0:h1, cols] = total[h0:].astype(bf16)
-                keep_y[k, g, 0:h0, cols] = total[:h0]
+                if h0:
+                    keep_y[k, g, 0:h0, cols] = total[:h0]
             else:
                 keep_o[g, 0:h0 + h1, cols] = total
 
         each_tile(s, 2 * kind + 1, body)
+        if h0 and kind in (DIAG, ZN):
+            z1_copy(s, kind).start()
         if kind == DIAG:
-            z1_copy(s, 0).start()
             y1_copy(s, 0).start()
-        elif kind == ZN:
-            z1_copy(s, 1).start()
         elif kind == YN:
             y1_copy(s, 1).start()
 
@@ -277,12 +290,12 @@
 
         lax.fori_loop(0, 2 * ncol, step, 0)
 
-    def relay(s):
-        k = s % 2
-        h0, h1 = halves[s], others[s]
-        if s >= 2:
+    def relay_y(s):
+        k, h0 = s % 2, halves[s]
+        if s >= 2 and halves[s - 2]:
             y2_copy(s - 2).wait_send()
-            z2_copy(s - 2).wait_send()
+        if h0 == 0:
+            return
         z1_copy(s, 0).wait_recv()
 
         def to_y2(g, cols):
@@ -291,6 +304,11 @@
 
         loop_cols(to_y2)
         y2_copy(s).start()
+
+    def relay_z(s):
+        k, h1 = s % 2, others[s]
+        if s >= 2:
+            z2_copy(s - 2).wait_send()
         y1_copy(s, 0).wait_recv()
 
         def to_z2(g, cols):
@@ -300,24 +318,29 @@
         loop_cols(to_z2)
         z2_copy(s).start()
 
+    def relay(s):
+        for step in (relay_z, relay_y) if Z_FIRST else (relay_y, relay_z):
+            step(s)
+
     def hid_copy(s):
         r = span(s)
-        return remote(hid.at[r], hid_in.at[r], hid_s.at[s], hid_r.at[s], to_a)
+        return remote(hid.at[r], hid_in.at[r], hid_s, hid_r.at[s], to_a)
 
     def finish(s):
         own(s, OWN)
-        z1_copy(s, 1).wait_recv()
         y1_copy(s, 1).wait_recv()
-        y2_copy(s).wait_recv()
+        if halves[s]:
+            z1_copy(s, 1).wait_recv()
+            y2_copy(s).wait_recv()
         z2_copy(s).wait_recv()
         h0, rows = halves[s], plan[s]
 
         def step(t, carry):
             cols = pl.ds(pl.multiple_of(t * col, 128), col)
-            for low, high, first, second in (
-                (0, h0, z1_in.at[1, :, z_span(s)], y2_in.at[:, z_span(s)]),
-                (h0, rows, y1_in.at[1, :, y_span(s)], z2_in.at[:, y_span(s)]),
-            ):
+            pieces = [(h0, rows, y1_in.at[1, :, y_span(s)], z2_in.at[:, y_span(s)])]
+            if h0:
+                pieces.append((0, h0, z1_in.at[1, :, z_span(s)], y2_in.at[:, z_span(s)]))
+            for low, high, first, second in pieces:
                 g, u = (
                     keep_o[i, low:high, cols] + first[i, :, cols].astype(f32) + second[i, :, cols].astype(f32)
                     for i in (0, 1)
@@ -329,78 +352,93 @@
         hid_copy(s).start()
 
     full = acc.shape[1]
-    dcol = tile_of(full)
+    part = full // 2
     dwidth = blocks.shape[2]
 
-    def dsib_copy(s, kind):
+    def dsib_copy(s, side):
+        near = pl.ds(2 * side, 2)
         r = span(s)
-        return remote(
-            dsib_out.at[kind, r], dsib_in.at[kind, r], dsib_s.at[s, kind], dsib_r.at[s, kind], to_c
-        )
+        return remote(dsib_out.at[near, r], dsib_in.at[near, r], dsib_s, dsib_r.at[s, side], to_c)
 
     def dout_copy(s, kind):
         r = span(s)
-        target = (to_d, to_z, to_y)[kind]
-        return remote(dout.at[kind, r], din.at[kind, r], dout_s.at[s, kind], dout_r.at[s, kind], target)
-
-    def project(s):
-        rows = plan[s]
+        target = (to_y if s < RELAYED else to_d, to_z, to_y)[kind]
+        return remote(dout.at[kind, r], din.at[kind, r], dout_s, dout_r.at[s, kind], target)
+
+    def base_of(s):
+        return plan[s - 1] if s == last else 0
+
+    def project_own(s):
+        rows, base = plan[s], base_of(s)
         if s == 0:
             down_copy.wait()
         first = pl.ds(pl.multiple_of(a * width, 128), width)
+        mine = hid.at[span(s), :]
+
+        acc[base:base + rows, :] = jnp.dot(mine[...], wd[first, :], preferred_element_type=f32)
+
+    def project_other(s):
+        rows, base = plan[s], base_of(s)
         second = pl.ds(pl.multiple_of((1 - a) * width, 128), width)
-        mine, theirs = hid.at[span(s), :], hid_in.at[span(s), :]
-
-        def own_half(t, carry):
-            cols = pl.ds(pl.multiple_of(t * dcol, 128), dcol)
-            acc[0:rows, cols] = jnp.dot(mine[...], wd[first, cols], preferred_element_type=f32)
-            return carry
-
-        lax.fori_loop(0, full // dcol, own_half, 0)
+        theirs = hid_in.at[span(s), :]
         hid_copy(s).wait_recv()
-
-        def other_half(t, carry):
-            cols = pl.ds(pl.multiple_of(t * dcol, 128), dcol)
-            acc[0:rows, cols] += jnp.dot(theirs[...], wd[second, cols], preferred_element_type=f32)
-            return carry
-
-        lax.fori_loop(0, full // dcol, other_half, 0)
-        for b in range(XS):
-            blocks[b, 0:rows] = acc[0:rows, b * dwidth:(b + 1) * dwidth]
-        for kind in range(4):
-            dsib_out[kind, span(s)] = blocks[block_of(kind, 1 - c), 0:rows].astype(bf16)
-            dsib_copy(s, kind).start()
+        for near, side in enumerate((1 - zb, zb)):
+            cols = pl.ds(pl.multiple_of(side * part, 128), part)
+            total = acc[base:base + rows, cols] + jnp.dot(
+                theirs[...], wd[second, cols], preferred_element_type=f32
+            )
+            for b in range(XS // 2):
+                blocks[side * (XS // 2) + b, 0:rows] = total[:, b * dwidth:(b + 1) * dwidth]
+            for kind in (2 * near, 2 * near + 1):
+                dsib_out[kind, span(s)] = blocks[block_of(kind, 1 - c), 0:rows].astype(bf16)
+            dsib_copy(s, near).start()
+
+    def project(s):
+        project_own(s)
+        project_other(s)
 
     def spread(s):
-        for kind in range(4):
-            dsib_copy(s, kind).wait_recv()
+        for kind in (DIAG, ZN, YN, OWN):
+            if kind in (DIAG, YN):
+                dsib_copy(s, kind // 2).wait_recv()
             total = blocks[block_of(kind, c), 0:plan[s]] + dsib_in[kind, span(s)].astype(f32)
             if kind == OWN:
                 keep_d[span(s)] = total
+            elif kind == ZN and s < RELAYED:
+                keep_n[span(s)] = total
             else:
                 dout[kind, span(s)] = total.astype(bf16)
 
     def send_out(s):
-        for kind in range(3):
+        for kind in (DIAG, YN) if s < RELAYED else (DIAG, YN, ZN):
             dout_copy(s, kind).start()
+
+    def relay_out(s):
+        dout_copy(s, DIAG).wait_recv()
+        total = keep_n[span(s)] + din[DIAG, span(s)].astype(f32)
+        dout[ZN, span(s)] = total.astype(bf16)
+        dout_copy(s, ZN).start()
+
+    def relay_outs(s):
+        if s < RELAYED:
+            relay_out(s)
 
     def collect(s):
         total = keep_d[span(s)]
-        for kind in range(3):
+        for kind in (YN, ZN) if s < RELAYED else (YN, ZN, DIAG):
             dout_copy(s, kind).wait_recv()
             total = total + din[kind, span(s)].astype(f32)
         keep_d[span(s)] = total
 
-    last = chunks - 1
     tok_copy(0).start()
     join(0)
-    for kind in (DIAG, ZN, YN):
-        sibling(0, kind)
+    sibling(0, DIAG)
+    sibling(0, ZN)
     own(0, DIAG)
+    sibling(0, YN)
+    own(0, ZN)
     sibling(0, OWN)
-    own(0, ZN)
     own(0, YN)
-    projected = 0
     for s in range(chunks):
         if s > 0:
             for kind in range(3):
@@ -410,23 +448,28 @@
             for kind in range(4):
                 sibling(s + 1, kind)
         if s >= 3:
-            project(projected)
+            project(s - 3)
         if s > 0:
             finish(s - 1)
         if s >= 3:
-            spread(projected)
-            projected += 1
+            spread(s - 3)
         relay(s)
-    for s in range(projected):
+    for s in range(last - 2):
         send_out(s)
-    while projected < last:
-        project(projected)
-        if projected == last - 2 or last < 2:
-            finish(last)
-        spread(projected)
-        send_out(projected)
-        projected += 1
-    project(last)
+    project(last - 2)
+    project_own(last - 1)
+    for s in range(last - 3):
+        relay_outs(s)
+    finish(last)
+    spread(last - 2)
+    send_out(last - 2)
+    relay_outs(last - 3)
+    project_other(last - 1)
+    project_own(last)
+    spread(last - 1)
+    send_out(last - 1)
+    relay_outs(last - 2)
+    project_other(last)
     spread(last)
     send_out(last)
     for s in range(chunks):
@@ -436,20 +479,18 @@
     out_copy = pltpu.make_async_copy(done, out_t, out_sem)
     out_copy.start()
 
-    for s in range(chunks):
-        tok_copy(s).wait_send()
-        hid_copy(s).wait_send()
-        for kind in range(4):
-            if s == last:
-                sib_copy(s, kind).wait_send()
-            dsib_copy(s, kind).wait_send()
-        for kind in range(3):
-            dout_copy(s, kind).wait_send()
-        if s >= chunks - 2:
-            for piece in range(2):
+    for buffer, sem, target in (
+        (tok, tok_s, to_a), (hid, hid_s, to_a), (dsib_out, dsib_s, to_c), (dout, dout_s, to_y)
+    ):
+        remote(buffer, buffer, sem, out_sem, target).wait_send()
+    sib_copy(last, 0).wait_send()
+    for s in range(max(chunks - 2, 0), chunks):
+        for piece in range(2):
+            if halves[s]:
                 z1_copy(s, piece).wait_send()
-                y1_copy(s, piece).wait_send()
-            z2_copy(s).wait_send()
+            y1_copy(s, piece).wait_send()
+        z2_copy(s).wait_send()
+        if halves[s]:
             y2_copy(s).wait_send()
     out_copy.wait()
 
@@ -457,7 +498,7 @@
 def plan_of(count):
     unit = count // sum(PLAN)
     plan = [unit * parts for parts in PLAN]
-    halves = [unit // 2 * parts for parts in Z_ROWS]
+    halves = [unit * parts for parts in Z_ROWS]
     return plan, halves
 
 
@@ -494,8 +535,9 @@
         v((2, rows, width), f32),
         v((count, width), bf16),
         v((count, width), bf16),
-        v((rows, full), f32),
+        v((max(rows, plan[-2] + plan[-1]), full), f32),
         v((XS, rows, dwidth), f32),
+        v((count, dwidth), f32),
         v((count, dwidth), f32),
         v((4, count, dwidth), bf16),
         v((4, count, dwidth), bf16),
@@ -505,8 +547,8 @@
     ]
     sem = pltpu.SemaphoreType.DMA
     s = len(plan)
-    shapes = [None, (s,), (s,), (2, XS), None, (s, 4), (s, 4), (s, 2), (s, 2), (s, 2), (s, 2)]
-    shapes += [(s,)] * 6 + [(s, 4), (s, 4), (s, 3), (s, 3), None]
+    shapes = [None, None, (s,), (XS,), None, (5,), (s + 3,), (2, 2), (s, 2), (2, 2), (s, 2)]
+    shapes += [(2,), (s,), (2,), (s,), None, (s,), None, (s, 2), None, (s, 3), None]
     sems = [sem if shape is None else sem(shape) for shape in shapes]
     hbm = pl.BlockSpec(memory_space=pl.ANY)
     result = pl.pallas_call(
@@ -527,8 +569,8 @@
     suits = (
         lax.axis_size("gx") == 2 * XS
         and width % 128 == 0
-        and down_weight.shape[2] % 128 == 0
-        and tokens.shape[0] % (32 * sum(PLAN)) == 0
+        and down_weight.shape[2] % 256 == 0
+        and tokens.shape[0] % (16 * sum(PLAN)) == 0
         and tokens.shape[0] % 128 == 0
         and tokens.shape[1] % 16 == 0
         and tokens.shape[1] == down_weight.shape[2] // XS

time: 106 us -> 99.4 us (0.938)
  Pallas kernels: 104 us -> 97.6 us
    pallas_call x1, Pallas kernels: 104 us -> 97.6 us  [fused(): pl.pallas_call(functools.partial(kernel, plan, halves), out_shape=jax.Sha...]
where the time goes in v2:
time: 99.4 us; the launch traced here: 99.3 us
  Pallas kernels  97.6 us (98%)
  local copies, waits for them, and re-layouts  1.64 us (2%)
    pallas_call x1, Pallas kernels, fused(): pl.pallas_call(functools.partial(kernel, plan, halves), out_shape=jax.Sha...  97.6 us

profile of v2, /device:TPU:0, one launch (start us, length us, event | category | flops | bytes accessed | tf_op | source)
XLA Modules:
  0.0 99.3 jit_solution(5186344617465190637)
XLA Ops:
  0.0 97.6 %shard_map.46 = bf16[288,384]{1,0:T(8,128)(2,1)} custom-call(bf16[288,384]{1,0:T(8,128)(2,1)} %bitcast.3, bf16[1,576,9216]{2,1,0:T(8,128)(2,1)} %gate.1, bf16[1,576,9216]{2,1,0:T(8,128)(2,1)} %up.1, bf16[1,2304,2304]{2,1,0:T(8,128)(2,1)} %down.1), custom_call_target="tpu_custom_call" | custom-call | tf_op jit(solution)/shard_map/pallas_call | solution.py:554
  97.6 1.6 %copy.6 = bf16[384,288]{0,1:T(8,128)(2,1)} copy(bf16[384,288]{0,1:T(8,128)(2,1)} %bitcast.2) | data formatting | bytes 442368

commit v3 on v2

--- a/solution.py
+++ b/solution.py
@@ -11,7 +11,7 @@
 PLAN = (4, 7, 6, 5, 2)
 Z_ROWS = (2, 2, 2, 1, 0)
 RELAYED = 3
-Z_FIRST = True
+Z_FIRST = False
 VMEM_BYTES = 67043328
 MESH = pl.DeviceIdType.MESH
 DIAG, ZN, YN, OWN = 0, 1, 2, 3
@@ -466,23 +466,25 @@
     relay_outs(last - 3)
     project_other(last - 1)
     project_own(last)
+    relay_outs(last - 2)
     spread(last - 1)
     send_out(last - 1)
-    relay_outs(last - 2)
     project_other(last)
     spread(last)
     send_out(last)
+    out_copies = []
     for s in range(chunks):
         collect(s)
-    for first in range(0, count, 128):
-        done[:, first:first + 128] = keep_d[first:first + 128, :].T.astype(bf16)
-    out_copy = pltpu.make_async_copy(done, out_t, out_sem)
-    out_copy.start()
-
+        while 128 * (len(out_copies) + 1) <= starts[s] + plan[s]:
+            index = len(out_copies)
+            block = pl.ds(128 * index, 128)
+            done[:, block] = keep_d[block, :].T.astype(bf16)
+            out_copies.append(pltpu.make_async_copy(done.at[:, block], out_t.at[:, block], out_sem.at[index]))
+            out_copies[index].start()
     for buffer, sem, target in (
         (tok, tok_s, to_a), (hid, hid_s, to_a), (dsib_out, dsib_s, to_c), (dout, dout_s, to_y)
     ):
-        remote(buffer, buffer, sem, out_sem, target).wait_send()
+        remote(buffer, buffer, sem, raw_sem, target).wait_send()
     sib_copy(last, 0).wait_send()
     for s in range(max(chunks - 2, 0), chunks):
         for piece in range(2):
@@ -492,7 +494,8 @@
         z2_copy(s).wait_send()
         if halves[s]:
             y2_copy(s).wait_send()
-    out_copy.wait()
+    for copy in out_copies:
+        copy.wait()
 
 
 def plan_of(count):
@@ -548,7 +551,7 @@
     sem = pltpu.SemaphoreType.DMA
     s = len(plan)
     shapes = [None, None, (s,), (XS,), None, (5,), (s + 3,), (2, 2), (s, 2), (2, 2), (s, 2)]
-    shapes += [(2,), (s,), (2,), (s,), None, (s,), None, (s, 2), None, (s, 3), None]
+    shapes += [(2,), (s,), (2,), (s,), None, (s,), None, (s, 2), None, (s, 3), (count // 128,)]
     sems = [sem if shape is None else sem(shape) for shape in shapes]
     hbm = pl.BlockSpec(memory_space=pl.ANY)
     result = pl.pallas_call(

time: 99.4 us -> 99.3 us (level)
  no operation moved by 1% of the time
where the time goes in v3:
time: 99.3 us; the launch traced here: 99.1 us
  Pallas kernels  97.5 us (98%)
  local copies, waits for them, and re-layouts  1.64 us (2%)
    pallas_call x1, Pallas kernels, fused(): pl.pallas_call(functools.partial(kernel, plan, halves), out_shape=jax.Sha...  97.5 us

profile of v3, /device:TPU:0, one launch (start us, length us, event | category | flops | bytes accessed | tf_op | source)
XLA Modules:
  0.0 99.1 jit_solution(16533549307121463575)
XLA Ops:
  0.0 97.5 %shard_map.46 = bf16[288,384]{1,0:T(8,128)(2,1)} custom-call(bf16[288,384]{1,0:T(8,128)(2,1)} %bitcast.3, bf16[1,576,9216]{2,1,0:T(8,128)(2,1)} %gate.1, bf16[1,576,9216]{2,1,0:T(8,128)(2,1)} %up.1, bf16[1,2304,2304]{2,1,0:T(8,128)(2,1)} %down.1), custom_call_target="tpu_custom_call" | custom-call | tf_op jit(solution)/shard_map/pallas_call | solution.py:557
  97.5 1.6 %copy.6 = bf16[384,288]{0,1:T(8,128)(2,1)} copy(bf16[384,288]{0,1:T(8,128)(2,1)} %bitcast.2) | data formatting | bytes 442368
